TPU v7x, 32 devices: a whole 2x2x4 slice. The times are simulated.
32 devices in a mesh: ocn: 4 (over z), grp: 8 (over y, x, core).
Axes of the slice: x: 2, y: 2, z: 4, core: 2. Of those that a mesh axis runs over, the one named last changes fastest.
Arguments:
- tracers: float32 [2, 32, 256, 1024], P(None, None, 'grp', 'ocn'), may hold values from -6 to 6
- velocity: float32 [2, 32, 256, 1024], P(None, None, 'grp', 'ocn'), may hold values from -3 to 3
- remap_weights: bfloat16 [256, 8, 128, 128], P('grp'), may hold values from -0.25 to 0.25
- remap_blocks: int32 [256, 8], P('grp'), may hold values from 0 to 2047
- remap_count: int32 [256], P('grp'), may hold values from 1 to 8, as said below
- ice_velocity: float32 [2, 32768], P(None, 'grp'), may hold values from -3 to 3
- ice_mass_rate: float32 [32768], P('grp'), may hold values from 0.5 to 4
- ice_strength: float32 [32768], P('grp'), may hold values from 0.5 to 8
- wind_stress: float32 [2, 32768], P(None, 'grp'), may hold values from -6 to 6
Outputs:
- tracers_next: float32 [2, 32, 256, 1024], P(None, None, 'grp', 'ocn')
- surface_flux: float32 [3, 256, 1024], P(None, 'grp', 'ocn')
- ice_final: float32 [2, 32768], P(None, 'grp')
Inputs may be any that keep to these rules, and one draw needn't show every extreme that they name: `remap_count`: every ice block has at least one live entry. The ice blocks of the first and of the last index of grp have 7 or 8 live entries; all others have 1 or 2.
All inputs are finite; a program needn't handle non-finite values.
Results may differ from a plain program's by a relative error of at most 0.0006.
The roundings to bfloat16 on the way count: a program that leaves them out, or rounds other values in their place, can miss the bound.
Values may be sent and summed in bfloat16 or wider, within the bound.
No kernel may reach another device: no remote copies, remote signals or barrier semaphores. Data moves between devices by JAX's collectives and lax.ppermute only.
A program may use at most 128 MiB of HBM per device.

v0:
```python
import jax
import jax.numpy as jnp
from jax import lax
from jax.sharding import PartitionSpec as P

BS = 128
K = 8
ITERS = 4
DEPTH = 3


def padded_2(block, sides, width):
    for axis, dim in sides:
        count = lax.axis_size(axis)
        forward = [(i, i + 1) for i in range(count - 1)]
        backward = [(target, source) for source, target in forward]
        low = lax.ppermute(
            lax.slice_in_dim(block, block.shape[dim] - width, None, axis=dim), axis, forward
        )
        high = lax.ppermute(lax.slice_in_dim(block, 0, width, axis=dim), axis, backward)
        block = jnp.concatenate([low, block, high], axis=dim)
    return block


def on_device(
    tracers,
    velocity,
    remap_weights,
    remap_blocks,
    remap_count,
    ice_velocity,
    ice_mass_rate,
    ice_strength,
    wind_stress,
):
    n_grp = lax.axis_size("grp")
    column = lax.axis_index("ocn")
    height = tracers.shape[2]
    across = tracers.shape[3]
    block_count = height * across // BS
    ice_blocks = remap_count.shape[0]
    entries = ice_blocks * K
    blocks_flat = remap_blocks.reshape(-1)
    valid = (jnp.arange(K)[None, :] < remap_count[:, None]).reshape(-1)
    owner_column = blocks_flat // (n_grp * block_count)
    local_rows = blocks_flat % (n_grp * block_count)
    mine = valid & (owner_column == column)
    weights = remap_weights.reshape(entries, BS, BS)
    surface = jnp.stack([tracers[0, 0], tracers[1, 0], velocity[0, 0], velocity[1, 0]]).astype(
        jnp.bfloat16
    )
    surface = surface.reshape(4, block_count, BS).transpose(1, 0, 2).reshape(block_count, 4 * BS)
    piece = lax.all_gather(surface, ("ocn", "grp"), axis=0, tiled=True)
    hits = (blocks_flat[:, None] == jnp.arange(piece.shape[0])[None, :]) & valid[:, None]
    chosen = jnp.dot(hits.astype(jnp.bfloat16), piece, preferred_element_type=jnp.float32)
    source = chosen.astype(jnp.bfloat16).reshape(entries, 4, BS)
    result = jnp.einsum("eij,efj->efi", weights, source, preferred_element_type=jnp.float32)
    remapped = result.reshape(ice_blocks, K, 4, BS).sum(axis=1)
    fields = remapped.transpose(1, 0, 2).reshape(4, ice_blocks * BS)
    ocean_current = fields[2:4]
    base = ice_mass_rate * ice_velocity + wind_stress + ocean_current
    total = 2.0 * ice_velocity.shape[1] * n_grp
    current = ice_velocity
    gvals = []
    fvals = []
    for step in range(ITERS):
        relax_padded = padded_2(current, (("grp", 1),), 1)
        left = relax_padded[:, :-2]
        right = relax_padded[:, 2:]
        strain = 0.5 * (right - left)
        zeta = ice_strength / (2.0 * jnp.sqrt(jnp.sum(strain * strain, axis=0) + 0.25))
        gnew = (base + zeta * (left + right)) / (ice_mass_rate + 1.0 + 2.0 * zeta)
        gvals.append(gnew)
        fvals.append(gnew - current)
        if step == 0:
            current = gnew
            continue
        depth = min(step, DEPTH)
        diffs = jnp.stack([fvals[j] - fvals[j - 1] for j in range(step - depth + 1, step + 1)])
        gdiffs = jnp.stack([gvals[j] - gvals[j - 1] for j in range(step - depth + 1, step + 1)])
        gram_local = jnp.einsum("aij,bij->ab", diffs, diffs, precision=lax.Precision.HIGHEST)
        rhs_local = jnp.einsum("aij,ij->a", diffs, fvals[step], precision=lax.Precision.HIGHEST)
        gram_raw, rhs_raw = lax.psum((gram_local, rhs_local), "grp")
        norms = jnp.sqrt(jnp.diagonal(gram_raw) / total + 1e-06)
        gram = gram_raw / total / (norms[:, None] * norms[None, :])
        rhs = rhs_raw / total / norms
        factor = jnp.linalg.cholesky(gram + 0.1 * jnp.eye(depth, dtype=jnp.float32))
        coef = jax.scipy.linalg.cho_solve((factor, True), rhs)
        current = gnew - jnp.einsum(
            "a,aij->ij", coef / norms, gdiffs, precision=lax.Precision.HIGHEST
        )
    heat = 0.5 * (-0.05 * fields[1] - fields[0])
    ice_flux = jnp.concatenate([current - ocean_current, heat[None]], axis=0).astype(jnp.bfloat16)
    flux_blocks = ice_flux.reshape(3, ice_blocks, BS).transpose(1, 0, 2)
    flux_entries = jnp.broadcast_to(flux_blocks[:, None], (ice_blocks, K, 3, BS)).reshape(
        entries, 3, BS
    )
    contrib = jnp.einsum("eij,efi->efj", weights, flux_entries, preferred_element_type=jnp.float32)
    contrib = contrib.reshape(entries, 3 * BS)
    hits = (jnp.arange(block_count * lax.axis_size("grp"))[:, None] == local_rows[None, :]) & mine[
        None, :
    ]
    returned = lax.psum_scatter(
        jnp.dot(hits.astype(jnp.float32), contrib, precision=lax.Precision.HIGHEST),
        "grp",
        scatter_dimension=0,
        tiled=True,
    )
    surface_flux = (
        returned.reshape(block_count, 3, BS).transpose(1, 0, 2).reshape(3, height, across)
    )
    padded = padded_2(tracers, (("ocn", 3), ("grp", 2)), 1)
    padded = jnp.pad(padded, ((0, 0), (1, 1), (0, 0), (0, 0)))
    centre = padded[:, 1:-1, 1:-1, 1:-1]
    east = padded[:, 1:-1, 1:-1, 2:]
    west = padded[:, 1:-1, 1:-1, :-2]
    north = padded[:, 1:-1, 2:, 1:-1]
    south = padded[:, 1:-1, :-2, 1:-1]
    upper = padded[:, :-2, 1:-1, 1:-1]
    lower = padded[:, 2:, 1:-1, 1:-1]
    advect = velocity[0][None] * (east - west) * 0.5 + velocity[1][None] * (north - south) * 0.5
    tracers_next = (
        centre
        + 0.2 * (east + west + north + south - 4.0 * centre)
        - 0.5 * advect
        + 0.2 * (upper + lower - 2.0 * centre)
    )
    tracers_next = tracers_next.at[0, 0].add(0.5 * surface_flux[2])
    return (tracers_next, surface_flux, current)


def solution(mesh):
    return jax.shard_map(
        on_device,
        mesh=mesh,
        in_specs=(
            P(None, None, "grp", "ocn"),
            P(None, None, "grp", "ocn"),
            P("grp", None, None, None),
            P("grp", None),
            P("grp"),
            P(None, "grp"),
            P("grp"),
            P("grp"),
            P(None, "grp"),
        ),
        out_specs=(P(None, None, "grp", "ocn"), P(None, "grp", "ocn"), P(None, "grp")),
        check_vma=False,
    )
```

profile of v0, /device:TPU:0, one launch (start us, length us, event | category | flops | bytes accessed | tf_op | source)
XLA Modules:
  0.0 221.9 jit_solution(3123802720105659784)
XLA Ops:
  7.2 1.9 convert.24
  11.8 1.7 copy.166
  15.2 5.6 %collective-permute-start.1 = (f32[2,32,32,1]{2,1,3,0:T(8,128)S(1)}, f32[2,32,32,1]{2,1,3,0:T(8,128)S(1)}, u32[]{:S(2)}, u32[]{:S(2)}) collective-permute-start(f32[2,32,32,1]{2,1,3,0:T(8,128)S(1)} %copy.167), channel_id=1, source_target_pairs={{0,8},{8,16},{16,24},{1,9},{9,17},{17,25},{2,10},{10,18},{18,26},{... | collective-permute-start | bytes 24584 | tf_op jit(solution)/shard_map/ppermute | solution.py:17
  22.2 3.2 %collective-permute-start.5 = (f32[2,1]{1,0:T(2,128)S(1)}, f32[2,1]{1,0:T(2,128)S(1)}, u32[]{:S(2)}, u32[]{:S(2)}) collective-permute-start(f32[2,1]{1,0:T(2,128)S(1)} %get-tuple-element.68), channel_id=1, source_target_pairs={{0,1},{1,2},{2,3},{3,4},{4,5},{5,6},{6,7},{8,9},{9,10},{10,11},{11... | collective-permute-start | bytes 32 | tf_op jit(solution)/shard_map/ppermute | solution.py:17
  25.4 2.8 %copy.120 = f32[2,32,32,256]{3,1,2,0:T(8,128)S(1)} copy(f32[2,32,32,256]{3,2,1,0:T(8,128)} %param.11) | data formatting | bytes 4194304 | tf_op args[0]
  28.5 1.6 copy.122
  30.1 1.6 copy.121
  36.0 1.8 copy.114
  40.7 29.1 %all-gather.2.cloned.1.call-done = bf16[2048,512]{1,0:T(8,128)(2,1)} async-done(((bf16[64,512]{1,0:T(8,128)(2,1)}), bf16[2048,512]{1,0:T(8,128)(2,1)}) %all-gather.2.cloned.1.call-update) | async-done | bytes 2097168 | tf_op jit(solution)/shard_map/all_gather | solution.py:53
  69.8 3.1 %fusion.7 = bf16[256,512]{1,0:T(8,128)(2,1)} fusion(bf16[2048,512]{1,0:T(8,128)(2,1)} %all-gather.2.cloned.1.call-done, s32[256]{0:T(256)S(1)} %reshape.286, pred[256]{0:T(512)(128)(4,1)S(1)} %lt.43), kind=kOutput, calls=%fused_computation.24 | convolution fusion | flops 538050560 | bytes 2360576 | tf_op jit(solution)/shard_map/dot_general | solution.py:55
  74.0 7.8 %bitcast_reduce_fusion = f32[32,4,128]{2,1,0:T(4,128)S(1)} fusion(bf16[256,4,128]{2,1,0:T(4,128)(2,1)S(1)} %reshape.288, bf16[256,128,128]{2,1,0:T(8,128)(2,1)} %bitcast.139), kind=kOutput, calls=%fused_computation.41 | convolution fusion | flops 33669120 | bytes 8716288 | tf_op jit(solution)/shard_map/eij,efj->efi/dot_general | solution.py:57
  83.4 3.0 %collective-permute-start.7 = (f32[2,1]{1,0:T(2,128)S(1)}, f32[2,1]{1,0:T(2,128)S(1)}, u32[]{:S(2)}, u32[]{:S(2)}) collective-permute-start(f32[2,1]{1,0:T(2,128)S(1)} %get-tuple-element.66), channel_id=1, source_target_pairs={{0,1},{1,2},{2,3},{3,4},{4,5},{5,6},{6,7},{8,9},{9,10},{10,11},{11... | collective-permute-start | bytes 32 | tf_op jit(solution)/shard_map/ppermute | solution.py:17
  88.3 14.7 %all-reduce.3 = (f32[1]{0:T(128)}, f32[1,1]{1,0:T(1,128)}) all-reduce(f32[1]{0:T(128)} %bitcast.6, f32[1,1]{1,0:T(1,128)} %bitcast.7), channel_id=1, replica_groups=mesh['ocn'=4,'grp'=8] {'grp'}, use_global_device_ids=true, to_apply=%region_3.4 | all-reduce | flops 2 | bytes 16 | tf_op jit(solution)/shard_map/psum | solution.py:83
  105.9 3.0 %collective-permute-start.9 = (f32[2,1]{1,0:T(2,128)S(1)}, f32[2,1]{1,0:T(2,128)S(1)}, u32[]{:S(2)}, u32[]{:S(2)}) collective-permute-start(f32[2,1]{1,0:T(2,128)S(1)} %get-tuple-element.64), channel_id=1, source_target_pairs={{0,1},{1,2},{2,3},{3,4},{4,5},{5,6},{6,7},{8,9},{9,10},{10,11},{11... | collective-permute-start | bytes 32 | tf_op jit(solution)/shard_map/ppermute | solution.py:17
  111.5 3.3 %collective-permute-start.3 = (f32[2,32,1,258]{3,1,2,0:T(8,128)}, f32[2,32,1,258]{3,1,2,0:T(8,128)}, u32[]{:S(2)}, u32[]{:S(2)}) collective-permute-start(f32[2,32,1,258]{3,1,2,0:T(8,128)} %get-tuple-element.50), channel_id=1, source_target_pairs={{0,1},{1,2},{2,3},{3,4},{4,5},{5,6},{6,7},{8,9},{9,10},{10,11},{11... | collective-permute-start | bytes 198152 | tf_op jit(solution)/shard_map/ppermute | solution.py:17
  114.8 14.7 %all-reduce.2 = (f32[2,2]{0,1:T(2,128)S(1)}, f32[2]{0:T(128)S(1)}) all-reduce(f32[2,2]{0,1:T(2,128)S(1)} %convolution_bitcast_fusion.1, f32[2]{0:T(128)S(1)} %convolution_bitcast_fusion.7), channel_id=1, replica_groups=mesh['ocn'=4,'grp'=8] {'grp'}, use_global_device_ids=true, to_apply=%region_6.7 | all-reduce | flops 6 | bytes 48 | tf_op jit(solution)/shard_map/psum | solution.py:83
  134.4 3.2 %collective-permute-start.11 = (f32[2,1]{1,0:T(2,128)S(1)}, f32[2,1]{1,0:T(2,128)S(1)}, u32[]{:S(2)}, u32[]{:S(2)}) collective-permute-start(f32[2,1]{1,0:T(2,128)S(1)} %get-tuple-element.62), channel_id=1, source_target_pairs={{0,1},{1,2},{2,3},{3,4},{4,5},{5,6},{6,7},{8,9},{9,10},{10,11},{11... | collective-permute-start | bytes 32 | tf_op jit(solution)/shard_map/ppermute | solution.py:17
  141.7 14.3 %all-reduce.1 = (f32[3,3]{0,1:T(4,128)S(1)}, f32[3]{0:T(128)S(1)}) all-reduce(f32[3,3]{0,1:T(4,128)S(1)} %convolution_bitcast_fusion, f32[3]{0:T(128)S(1)} %convolution_bitcast_fusion.4), channel_id=1, replica_groups=mesh['ocn'=4,'grp'=8] {'grp'}, use_global_device_ids=true, to_apply=%region_11.12 | all-reduce | flops 12 | bytes 96 | tf_op jit(solution)/shard_map/psum | solution.py:83
  160.7 6.5 %fusion.56 = f32[256,3,128]{2,1,0:T(4,128)} fusion(bf16[256,3,128]{2,1,0:T(4,128)(2,1)S(1)} %bitcast.142, bf16[256,128,128]{2,1,0:T(8,128)(2,1)} %bitcast.140), kind=kOutput, calls=%fused_computation.162 | convolution fusion | flops 25165824 | bytes 8978432 | tf_op jit(solution)/shard_map/eij,efi->efj/dot_general | solution.py:98
  170.0 3.2 %select_maximum_fusion = f32[2,34,34,258]{3,1,2,0:T(8,128)S(1)} fusion(f32[2,32,1,258]{3,1,2,0:T(8,128)} %collective-permute-done.2, f32[2,32,1,258]{3,1,2,0:T(8,128)} %collective-permute-done.3, f32[2,32,32,1]{3,1,2,0:T(8,128)S(1)} %copy.112, f32[2,32,32,256]{3,1,2,0:T(8,128)S(1)} %copy.120, f32[2,32,32,1]{3,1,2,0:T(8,128)} %copy.114), kind=kLoop, calls=%fused_computation.4 | loop fusion | flops 7157952 | bytes 4631616 | tf_op jit(solution)/shard_map/concatenate | solution.py:21
  173.2 6.2 %fusion.3 = f32[2,32,32,256]{3,1,2,0:T(8,128)} fusion(f32[2,34,34,258]{3,1,2,0:T(8,128)S(1)} %select_maximum_fusion, f32[2,32,32,256]{3,1,2,0:T(8,128)S(1)} %copy.120, f32[2,32,32,1]{3,1,2,0:T(8,128)S(1)} %copy.112, f32[2,32,32,1]{3,1,2,0:T(8,128)S(1)} %copy-done.1, f32[2,32,1,258]{3,1,2,0:T(8,128)} %collective-permute-done.3, ...), kind=kLoop, calls=%fused_computation.12 | loop fusion | flops 14155776 | bytes 10634240 | tf_op jit(solution)/shard_map/add | solution.py:123
  179.4 27.1 %reduce-scatter.2.cloned.1.call-done = f32[64,384]{1,0:T(8,128)} async-done(((f32[512,384]{1,0:T(8,128)}), f32[64,384]{1,0:T(8,128)}) %reduce-scatter.2.cloned.1.call-update) | async-done | bytes 98320 | tf_op jit(solution)/shard_map/reduce_scatter | solution.py:103
  208.5 1.8 scatter-add.4
  210.3 4.1 %copy.148 = f32[2,32,32,256]{3,2,1,0:T(8,128)} copy(f32[2,32,32,256]{3,1,2,0:T(8,128)} %scatter-add.4) | data formatting | bytes 4194304
  (163 shorter events, 40.3 us)
Async XLA Ops:
  7.2 62.7 %all-gather.2.cloned.1.call-start = ((), (), s32[]{:S(2)}) async-start(), calls=%async_computation.1 | async-start | bytes 2162688 | tf_op jit(solution)/shard_map/all_gather | solution.py:53
  10.4 196.1 %reduce-scatter.2.cloned.1.call-start = ((), (), s32[]{:S(2)}) async-start(), calls=%async_computation.2 | async-start | bytes 884736 | tf_op jit(solution)/shard_map/reduce_scatter | solution.py:103
  11.8 9.0 %copy-start.6 = (f32[2,4096]{1,0:T(2,128)S(1)}, f32[2,4096]{1,0:T(2,128)}, u32[]{:S(2)}) copy-start(f32[2,4096]{1,0:T(2,128)} %param.16) | copy-start | bytes 98308
  13.5 21.6 %collective-permute-start = (f32[2,32,32,1]{2,1,3,0:T(8,128)S(1)}, f32[2,32,32,1]{2,1,3,0:T(8,128)S(1)}, u32[]{:S(2)}, u32[]{:S(2)}) collective-permute-start(f32[2,32,32,1]{2,1,3,0:T(8,128)S(1)} %copy.166), channel_id=1, source_target_pairs={{8,0},{16,8},{24,16},{9,1},{17,9},{25,17},{10,2},{18,10},{26,18},{... | collective-permute-start | bytes 24584 | tf_op jit(solution)/shard_map/ppermute | solution.py:20
  15.2 20.8 %collective-permute-start.1 = (f32[2,32,32,1]{2,1,3,0:T(8,128)S(1)}, f32[2,32,32,1]{2,1,3,0:T(8,128)S(1)}, u32[]{:S(2)}, u32[]{:S(2)}) collective-permute-start(f32[2,32,32,1]{2,1,3,0:T(8,128)S(1)} %copy.167), channel_id=1, source_target_pairs={{0,8},{8,16},{16,24},{1,9},{9,17},{17,25},{2,10},{10,18},{18,26},{... | collective-permute-start | bytes 24584 | tf_op jit(solution)/shard_map/ppermute | solution.py:17
  20.9 13.4 %collective-permute-start.4 = (f32[2,1]{1,0:T(2,128)S(1)}, f32[2,1]{1,0:T(2,128)S(1)}, u32[]{:S(2)}, u32[]{:S(2)}) collective-permute-start(f32[2,1]{1,0:T(2,128)S(1)} %get-tuple-element.69), channel_id=1, source_target_pairs={{1,0},{2,1},{3,2},{4,3},{5,4},{6,5},{7,6},{9,8},{10,9},{11,10},{12... | collective-permute-start | bytes 32 | tf_op jit(solution)/shard_map/ppermute | solution.py:20
  22.2 12.1 %collective-permute-start.5 = (f32[2,1]{1,0:T(2,128)S(1)}, f32[2,1]{1,0:T(2,128)S(1)}, u32[]{:S(2)}, u32[]{:S(2)}) collective-permute-start(f32[2,1]{1,0:T(2,128)S(1)} %get-tuple-element.68), channel_id=1, source_target_pairs={{0,1},{1,2},{2,3},{3,4},{4,5},{5,6},{6,7},{8,9},{9,10},{10,11},{11... | collective-permute-start | bytes 32 | tf_op jit(solution)/shard_map/ppermute | solution.py:17
  39.5 130.5 %collective-permute-start.2 = (f32[2,32,1,258]{3,1,2,0:T(8,128)}, f32[2,32,1,258]{3,1,2,0:T(8,128)}, u32[]{:S(2)}, u32[]{:S(2)}) collective-permute-start(f32[2,32,1,258]{3,1,2,0:T(8,128)} %get-tuple-element.51), channel_id=1, source_target_pairs={{1,0},{2,1},{3,2},{4,3},{5,4},{6,5},{7,6},{9,8},{10,9},{11,10},{12... | collective-permute-start | bytes 198152 | tf_op jit(solution)/shard_map/ppermute | solution.py:20
  73.9 7.9 %copy-start.8 = (f32[4096]{0:T(1024)S(1)}, f32[4096]{0:T(1024)}, u32[]{:S(2)}) copy-start(f32[4096]{0:T(1024)} %get-tuple-element.49) | copy-start | bytes 49156
  73.9 7.9 %copy-start.11 = (f32[2,4096]{1,0:T(2,128)S(1)}, f32[2,4096]{1,0:T(2,128)}, u32[]{:S(2)}) copy-start(f32[2,4096]{1,0:T(2,128)} %param.19) | copy-start | bytes 98308
  73.9 7.9 %copy-start.14 = (f32[2,1]{1,0:T(2,128)S(1)}, f32[2,1]{1,0:T(2,128)}, u32[]{:S(2)}) copy-start(f32[2,1]{1,0:T(2,128)} %copy-done.13) | copy-start | bytes 28
  74.0 7.9 %copy-start.16 = (f32[2,1]{1,0:T(2,128)S(1)}, f32[2,1]{1,0:T(2,128)}, u32[]{:S(2)}) copy-start(f32[2,1]{1,0:T(2,128)} %copy-done.15) | copy-start | bytes 28
  81.8 47.7 %copy-start.20 = (s32[2]{0:T(128)S(1)}, s32[2]{0:T(128)}, u32[]{:S(2)}) copy-start(s32[2]{0:T(128)} %or_bitcast_fusion.1) | copy-start | bytes 28
  82.0 74.0 %copy-start.12 = (s32[3]{0:T(128)S(1)}, s32[3]{0:T(128)}, u32[]{:S(2)}) copy-start(s32[3]{0:T(128)} %or_bitcast_fusion) | copy-start | bytes 40
  82.1 4.3 %collective-permute-start.6 = (f32[2,1]{1,0:T(2,128)S(1)}, f32[2,1]{1,0:T(2,128)S(1)}, u32[]{:S(2)}, u32[]{:S(2)}) collective-permute-start(f32[2,1]{1,0:T(2,128)S(1)} %get-tuple-element.67), channel_id=1, source_target_pairs={{1,0},{2,1},{3,2},{4,3},{5,4},{6,5},{7,6},{9,8},{10,9},{11,10},{12... | collective-permute-start | bytes 32 | tf_op jit(solution)/shard_map/ppermute | solution.py:20
  83.4 3.8 %collective-permute-start.7 = (f32[2,1]{1,0:T(2,128)S(1)}, f32[2,1]{1,0:T(2,128)S(1)}, u32[]{:S(2)}, u32[]{:S(2)}) collective-permute-start(f32[2,1]{1,0:T(2,128)S(1)} %get-tuple-element.66), channel_id=1, source_target_pairs={{0,1},{1,2},{2,3},{3,4},{4,5},{5,6},{6,7},{8,9},{9,10},{10,11},{11... | collective-permute-start | bytes 32 | tf_op jit(solution)/shard_map/ppermute | solution.py:17
  104.6 4.4 %collective-permute-start.8 = (f32[2,1]{1,0:T(2,128)S(1)}, f32[2,1]{1,0:T(2,128)S(1)}, u32[]{:S(2)}, u32[]{:S(2)}) collective-permute-start(f32[2,1]{1,0:T(2,128)S(1)} %get-tuple-element.65), channel_id=1, source_target_pairs={{1,0},{2,1},{3,2},{4,3},{5,4},{6,5},{7,6},{9,8},{10,9},{11,10},{12... | collective-permute-start | bytes 32 | tf_op jit(solution)/shard_map/ppermute | solution.py:20
  105.9 3.8 %collective-permute-start.9 = (f32[2,1]{1,0:T(2,128)S(1)}, f32[2,1]{1,0:T(2,128)S(1)}, u32[]{:S(2)}, u32[]{:S(2)}) collective-permute-start(f32[2,1]{1,0:T(2,128)S(1)} %get-tuple-element.64), channel_id=1, source_target_pairs={{0,1},{1,2},{2,3},{3,4},{4,5},{5,6},{6,7},{8,9},{9,10},{10,11},{11... | collective-permute-start | bytes 32 | tf_op jit(solution)/shard_map/ppermute | solution.py:17
  109.0 29.4 %copy-start.9 = (f32[1,2,4096]{2,0,1:T(1,128)}, f32[1,2,4096]{2,0,1:T(1,128)S(1)}, u32[]{:S(2)}) copy-start(f32[1,2,4096]{2,0,1:T(1,128)S(1)} %copy.130) | copy-start | bytes 98308
  111.5 58.5 %collective-permute-start.3 = (f32[2,32,1,258]{3,1,2,0:T(8,128)}, f32[2,32,1,258]{3,1,2,0:T(8,128)}, u32[]{:S(2)}, u32[]{:S(2)}) collective-permute-start(f32[2,32,1,258]{3,1,2,0:T(8,128)} %get-tuple-element.50), channel_id=1, source_target_pairs={{0,1},{1,2},{2,3},{3,4},{4,5},{5,6},{6,7},{8,9},{9,10},{10,11},{11... | collective-permute-start | bytes 198152 | tf_op jit(solution)/shard_map/ppermute | solution.py:17
  133.1 4.5 %collective-permute-start.10 = (f32[2,1]{1,0:T(2,128)S(1)}, f32[2,1]{1,0:T(2,128)S(1)}, u32[]{:S(2)}, u32[]{:S(2)}) collective-permute-start(f32[2,1]{1,0:T(2,128)S(1)} %get-tuple-element.63), channel_id=1, source_target_pairs={{1,0},{2,1},{3,2},{4,3},{5,4},{6,5},{7,6},{9,8},{10,9},{11,10},{12... | collective-permute-start | bytes 32 | tf_op jit(solution)/shard_map/ppermute | solution.py:20
  134.4 3.8 %collective-permute-start.11 = (f32[2,1]{1,0:T(2,128)S(1)}, f32[2,1]{1,0:T(2,128)S(1)}, u32[]{:S(2)}, u32[]{:S(2)}) collective-permute-start(f32[2,1]{1,0:T(2,128)S(1)} %get-tuple-element.62), channel_id=1, source_target_pairs={{0,1},{1,2},{2,3},{3,4},{4,5},{5,6},{6,7},{8,9},{9,10},{10,11},{11... | collective-permute-start | bytes 32 | tf_op jit(solution)/shard_map/ppermute | solution.py:17
  160.7 7.7 %copy-start.17 = (s32[256]{0:T(256)S(1)}, s32[256]{0:T(256)}, u32[]{:S(2)}) copy-start(s32[256]{0:T(256)} %and_select_fusion.1) | copy-start | bytes 3076
  160.7 7.7 %copy-start.19 = (pred[256]{0:T(512)(128)(4,1)S(1)}, pred[256]{0:T(512)(128)(4,1)}, u32[]{:S(2)}) copy-start(pred[256]{0:T(512)(128)(4,1)} %compare_and_fusion) | copy-start | bytes 772
  (12 other events, 48.4 us)
Sparse Core Ops, SparseCore 0:
  10.8 58.9 all-gather.1
  170.1 36.4 reduce-scatter.1
where the time goes:
time: 223 us; the launch traced here: 222 us
  waiting for transfers between devices  58.4 us (26%)
  blocking collectives  43.7 us (20%)
  starting transfers between devices  29.1 us (13%)
  local copies, waits for them, and re-layouts  25.8 us (12%)
  matrix products  24.6 us (11%)
  other arithmetic  24 us (11%)
  between operations  16.4 us (7%)
    psum x3, blocking collectives, on_device(): gram_raw, rhs_raw = lax.psum((gram_local, rhs_local), 'grp')  43.7 us
    all_gather x1, waiting for transfers between devices, on_device(): piece = lax.all_gather(surface, ('ocn', 'grp'), axis=0, tiled=True)  29.1 us
    reduce_scatter x1, waiting for transfers between devices, on_device(): lax.psum_scatter(jnp.dot(hits.astype(jnp.float32), contrib, precision=lax...  27.1 us
    ppermute x6, starting transfers between devices, padded_2(): lax.ppermute(lax.slice_in_dim(block, block.shape[dim] - width, None, axis...  21.3 us
    unnamed x52, local copies, waits for them, and re-layouts  10.1 us
    dot_general x1, matrix products, on_device(): jnp.einsum('eij,efj->efi', weights, source, preferred_element_type=jnp.fl...  7.84 us
    ppermute x6, starting transfers between devices, padded_2(): lax.ppermute(lax.slice_in_dim(block, 0, width, axis=dim), axis, backward)  7.7 us
    dot_general x1, matrix products, on_device(): jnp.einsum('eij,efi->efj', weights, flux_entries, preferred_element_type=...  6.46 us
  transfers between devices with their start and end apart: 14, of which 5 were waited for; matrix products, arithmetic and copies ran while one was open for 28% of the time, Pallas kernels for 0%

commit v1 on v0

--- a/solution.py
+++ b/solution.py
@@ -7,6 +7,23 @@
 K = 8
 ITERS = 4
 DEPTH = 3
+
+
+def joined_along(blocks, dim):
+    shape = list(blocks.shape[1:])
+    shape[dim] *= blocks.shape[0]
+    return jnp.moveaxis(blocks, 0, dim).reshape(shape)
+
+
+def doubled(x, axis):
+    count, index = (lax.axis_size(axis), lax.axis_index(axis))
+    pieces, stride = (x[None], 1)
+    while stride < count:
+        theirs = lax.ppermute(pieces, axis, [(i, i ^ stride) for i in range(count)])
+        low = index & stride == 0
+        pieces = jnp.concatenate([jnp.where(low, pieces, theirs), jnp.where(low, theirs, pieces)])
+        stride *= 2
+    return pieces
 
 
 def padded_2(block, sides, width):
@@ -50,7 +67,7 @@
         jnp.bfloat16
     )
     surface = surface.reshape(4, block_count, BS).transpose(1, 0, 2).reshape(block_count, 4 * BS)
-    piece = lax.all_gather(surface, ("ocn", "grp"), axis=0, tiled=True)
+    piece = joined_along(doubled(surface, ("ocn", "grp")), 0)
     hits = (blocks_flat[:, None] == jnp.arange(piece.shape[0])[None, :]) & valid[:, None]
     chosen = jnp.dot(hits.astype(jnp.bfloat16), piece, preferred_element_type=jnp.float32)
     source = chosen.astype(jnp.bfloat16).reshape(entries, 4, BS)

time: 223 us -> 249 us (1.12)
  waiting for transfers between devices: 58.4 us -> 70.5 us
  starting transfers between devices: 29.1 us -> 37 us
  other arithmetic: 24 us -> 29.9 us
    ppermute x0 -> x5, waiting for transfers between devices: none -> 39.7 us  [doubled(): theirs = lax.ppermute(pieces, axis, [(i, i ^ stride) for i in range(count)])]
    all_gather x1 -> x0, waiting for transfers between devices: 29.1 us -> none  [on_device(): piece = lax.all_gather(surface, ('ocn', 'grp'), axis=0, tiled=True)]
    ppermute x0 -> x5, starting transfers between devices: none -> 8.83 us  [doubled(): theirs = lax.ppermute(pieces, axis, [(i, i ^ stride) for i in range(count)])]
    select_n x0 -> x5, other arithmetic: none -> 3.57 us  [doubled(): jnp.where(low, pieces, theirs)]
    unnamed x52 -> x67, local copies, waits for them, and re-layouts: 10.1 us -> 9.88 us
  transfers between devices with their start and end apart: 14 -> 18, of which waited for: 5 -> 8; matrix products, arithmetic and copies ran while one was open for 28% -> 28% of each run, Pallas kernels for 0% -> 0%
where the time goes in v1:
time: 249 us; the launch traced here: 248 us
  waiting for transfers between devices  70.5 us (28%)
  blocking collectives  43.1 us (17%)
  starting transfers between devices  37 us (15%)
  other arithmetic  29.9 us (12%)
  local copies, waits for them, and re-layouts  27.8 us (11%)
  matrix products  23 us (9%)
  between operations  16.4 us (7%)
    psum x3, blocking collectives, on_device(): gram_raw, rhs_raw = lax.psum((gram_local, rhs_local), 'grp')  43.1 us
    ppermute x5, waiting for transfers between devices, doubled(): theirs = lax.ppermute(pieces, axis, [(i, i ^ stride) for i in range(count)])  39.7 us
    reduce_scatter x1, waiting for transfers between devices, on_device(): lax.psum_scatter(jnp.dot(hits.astype(jnp.float32), contrib, precision=lax...  28.7 us
    ppermute x6, starting transfers between devices, padded_2(): lax.ppermute(lax.slice_in_dim(block, block.shape[dim] - width, None, axis...  20.4 us
    unnamed x67, local copies, waits for them, and re-layouts  9.88 us
    ppermute x5, starting transfers between devices, doubled(): theirs = lax.ppermute(pieces, axis, [(i, i ^ stride) for i in range(count)])  8.83 us
    dot_general x1, matrix products, on_device(): jnp.einsum('eij,efj->efi', weights, source, preferred_element_type=jnp.fl...  7.84 us
    ppermute x6, starting transfers between devices, padded_2(): lax.ppermute(lax.slice_in_dim(block, 0, width, axis=dim), axis, backward)  7.68 us
  transfers between devices with their start and end apart: 18, of which 8 were waited for; matrix products, arithmetic and copies ran while one was open for 28% of the time, Pallas kernels for 0%

profile of v1, /device:TPU:0, one launch (start us, length us, event | category | flops | bytes accessed | tf_op | source)
XLA Modules:
  0.0 247.7 jit_solution(354206201576247294)
XLA Ops:
  7.2 1.9 convert.24
  11.3 2.9 %collective-permute-start.5 = (bf16[2,64,512]{2,1,0:T(8,128)(2,1)S(1)}, bf16[2,64,512]{2,1,0:T(8,128)(2,1)S(1)}, u32[]{:S(2)}, u32[]{:S(2)}) collective-permute-start(bf16[2,64,512]{2,1,0:T(8,128)(2,1)S(1)} %pad_maximum_fusion.12), channel_id=1, source_target_pairs={{0,2},{1,3},{2,0},{3,1},{4,6},{5,7},{6,4},{7,5},{8,10},{9,11},{10,... | collective-permute-start | bytes 393224 | tf_op jit(solution)/shard_map/ppermute | solution.py:22
  14.2 3.8 %collective-permute-done.5 = bf16[2,64,512]{2,1,0:T(8,128)(2,1)S(1)} collective-permute-done((bf16[2,64,512]{2,1,0:T(8,128)(2,1)S(1)}, bf16[2,64,512]{2,1,0:T(8,128)(2,1)S(1)}, u32[]{:S(2)}, u32[]{:S(2)}) %collective-permute-start.5) | collective-permute-done | bytes 131104 | tf_op jit(solution)/shard_map/ppermute | solution.py:22
  21.8 2.4 copy.166
  26.6 5.1 %collective-permute-start.1 = (f32[2,32,32,1]{2,1,3,0:T(8,128)}, f32[2,32,32,1]{2,1,3,0:T(8,128)}, u32[]{:S(2)}, u32[]{:S(2)}) collective-permute-start(f32[2,32,32,1]{2,1,3,0:T(8,128)} %copy.167), channel_id=1, source_target_pairs={{0,8},{8,16},{16,24},{1,9},{9,17},{17,25},{2,10},{10,18},{18,26},{... | collective-permute-start | bytes 24584 | tf_op jit(solution)/shard_map/ppermute | solution.py:34
  36.7 3.0 %collective-permute-start.10 = (f32[2,1]{1,0:T(2,128)S(1)}, f32[2,1]{1,0:T(2,128)S(1)}, u32[]{:S(2)}, u32[]{:S(2)}) collective-permute-start(f32[2,1]{1,0:T(2,128)S(1)} %get-tuple-element.78), channel_id=1, source_target_pairs={{0,1},{1,2},{2,3},{3,4},{4,5},{5,6},{6,7},{8,9},{9,10},{10,11},{11... | collective-permute-start | bytes 32 | tf_op jit(solution)/shard_map/ppermute | solution.py:34
  40.0 6.3 %collective-permute-done.7 = bf16[8,64,512]{2,1,0:T(8,128)(2,1)} collective-permute-done((bf16[8,64,512]{2,1,0:T(8,128)(2,1)}, bf16[8,64,512]{2,1,0:T(8,128)(2,1)}, u32[]{:S(2)}, u32[]{:S(2)}) %collective-permute-start.7) | collective-permute-done | bytes 524320 | tf_op jit(solution)/shard_map/ppermute | solution.py:22
  48.6 2.6 %collective-permute-start.8 = (bf16[16,64,512]{2,1,0:T(8,128)(2,1)}, bf16[16,64,512]{2,1,0:T(8,128)(2,1)}, u32[]{:S(2)}, u32[]{:S(2)}) collective-permute-start(bf16[16,64,512]{2,1,0:T(8,128)(2,1)} %pad_maximum_fusion.9), channel_id=1, source_target_pairs={{0,16},{1,17},{2,18},{3,19},{4,20},{5,21},{6,22},{7,23},{8,24},{9,... | collective-permute-start | bytes 3145736 | tf_op jit(solution)/shard_map/ppermute | solution.py:22
  60.7 2.6 %copy.114 = f32[2,32,32,1]{3,1,2,0:T(8,128)} copy(f32[2,32,32,1]{2,1,3,0:T(8,128)} %collective-permute-done.1) | data formatting | bytes 16384 | tf_op jit(solution)/shard_map/ppermute | solution.py:34
  66.2 28.7 %collective-permute-done.8 = bf16[16,64,512]{2,1,0:T(8,128)(2,1)} collective-permute-done((bf16[16,64,512]{2,1,0:T(8,128)(2,1)}, bf16[16,64,512]{2,1,0:T(8,128)(2,1)}, u32[]{:S(2)}, u32[]{:S(2)}) %collective-permute-start.8) | collective-permute-done | bytes 1048608 | tf_op jit(solution)/shard_map/ppermute | solution.py:22
  99.0 7.8 %bitcast_reduce_fusion = f32[32,4,128]{2,1,0:T(4,128)S(1)} fusion(bf16[256,4,128]{2,1,0:T(4,128)(2,1)S(1)} %reshape.288, bf16[256,128,128]{2,1,0:T(8,128)(2,1)} %bitcast.137), kind=kOutput, calls=%fused_computation.46 | convolution fusion | flops 33669120 | bytes 8716288 | tf_op jit(solution)/shard_map/eij,efj->efi/dot_general | solution.py:74
  108.5 3.0 %collective-permute-start.12 = (f32[2,1]{1,0:T(2,128)S(1)}, f32[2,1]{1,0:T(2,128)S(1)}, u32[]{:S(2)}, u32[]{:S(2)}) collective-permute-start(f32[2,1]{1,0:T(2,128)S(1)} %get-tuple-element.76), channel_id=1, source_target_pairs={{0,1},{1,2},{2,3},{3,4},{4,5},{5,6},{6,7},{8,9},{9,10},{10,11},{11... | collective-permute-start | bytes 32 | tf_op jit(solution)/shard_map/ppermute | solution.py:34
  113.2 13.8 %all-reduce.3 = (f32[1]{0:T(128)}, f32[1,1]{1,0:T(1,128)}) all-reduce(f32[1]{0:T(128)} %bitcast.7, f32[1,1]{1,0:T(1,128)} %bitcast.8), channel_id=1, replica_groups=mesh['ocn'=4,'grp'=8] {'grp'}, use_global_device_ids=true, to_apply=%region_3.4 | all-reduce | flops 2 | bytes 16 | tf_op jit(solution)/shard_map/psum | solution.py:100
  129.9 3.2 %collective-permute-start.14 = (f32[2,1]{1,0:T(2,128)S(1)}, f32[2,1]{1,0:T(2,128)S(1)}, u32[]{:S(2)}, u32[]{:S(2)}) collective-permute-start(f32[2,1]{1,0:T(2,128)S(1)} %get-tuple-element.74), channel_id=1, source_target_pairs={{0,1},{1,2},{2,3},{3,4},{4,5},{5,6},{6,7},{8,9},{9,10},{10,11},{11... | collective-permute-start | bytes 32 | tf_op jit(solution)/shard_map/ppermute | solution.py:34
  135.5 3.0 %collective-permute-start.3 = (f32[2,32,1,258]{3,1,2,0:T(8,128)}, f32[2,32,1,258]{3,1,2,0:T(8,128)}, u32[]{:S(2)}, u32[]{:S(2)}) collective-permute-start(f32[2,32,1,258]{3,1,2,0:T(8,128)} %get-tuple-element.50), channel_id=1, source_target_pairs={{0,1},{1,2},{2,3},{3,4},{4,5},{5,6},{6,7},{8,9},{9,10},{10,11},{11... | collective-permute-start | bytes 198152 | tf_op jit(solution)/shard_map/ppermute | solution.py:34
  138.5 15.0 %all-reduce.2 = (f32[2,2]{0,1:T(2,128)S(1)}, f32[2]{0:T(128)S(1)}) all-reduce(f32[2,2]{0,1:T(2,128)S(1)} %convolution_bitcast_fusion.1, f32[2]{0:T(128)S(1)} %convolution_bitcast_fusion.7), channel_id=1, replica_groups=mesh['ocn'=4,'grp'=8] {'grp'}, use_global_device_ids=true, to_apply=%region_6.7 | all-reduce | flops 6 | bytes 48 | tf_op jit(solution)/shard_map/psum | solution.py:100
  158.5 3.0 %collective-permute-start.16 = (f32[2,1]{1,0:T(2,128)S(1)}, f32[2,1]{1,0:T(2,128)S(1)}, u32[]{:S(2)}, u32[]{:S(2)}) collective-permute-start(f32[2,1]{1,0:T(2,128)S(1)} %get-tuple-element.72), channel_id=1, source_target_pairs={{0,1},{1,2},{2,3},{3,4},{4,5},{5,6},{6,7},{8,9},{9,10},{10,11},{11... | collective-permute-start | bytes 32 | tf_op jit(solution)/shard_map/ppermute | solution.py:34
  165.8 14.3 %all-reduce.1 = (f32[3,3]{0,1:T(4,128)S(1)}, f32[3]{0:T(128)S(1)}) all-reduce(f32[3,3]{0,1:T(4,128)S(1)} %convolution_bitcast_fusion, f32[3]{0:T(128)S(1)} %convolution_bitcast_fusion.4), channel_id=1, replica_groups=mesh['ocn'=4,'grp'=8] {'grp'}, use_global_device_ids=true, to_apply=%region_11.12 | all-reduce | flops 12 | bytes 96 | tf_op jit(solution)/shard_map/psum | solution.py:100
  184.8 6.5 %fusion.56 = f32[256,3,128]{2,1,0:T(4,128)} fusion(bf16[256,3,128]{2,1,0:T(4,128)(2,1)S(1)} %bitcast.141, bf16[256,128,128]{2,1,0:T(8,128)(2,1)} %bitcast.138), kind=kOutput, calls=%fused_computation.176 | convolution fusion | flops 25165824 | bytes 8978432 | tf_op jit(solution)/shard_map/eij,efi->efj/dot_general | solution.py:115
  194.1 3.2 %select_maximum_fusion = f32[2,34,34,258]{3,1,2,0:T(8,128)S(1)} fusion(f32[2,32,1,258]{3,1,2,0:T(8,128)} %collective-permute-done.2, f32[2,32,1,258]{3,1,2,0:T(8,128)} %collective-permute-done.3, f32[2,32,32,1]{3,1,2,0:T(8,128)S(1)} %copy.112, f32[2,32,32,256]{3,1,2,0:T(8,128)S(1)} %copy.120, f32[2,32,32,1]{3,1,2,0:T(8,128)} %copy.114), kind=kLoop, calls=%fused_computation.4 | loop fusion | flops 7157952 | bytes 4631616 | tf_op jit(solution)/shard_map/concatenate | solution.py:38
  197.3 6.2 %fusion.3 = f32[2,32,32,256]{3,1,2,0:T(8,128)} fusion(f32[2,34,34,258]{3,1,2,0:T(8,128)S(1)} %select_maximum_fusion, f32[2,32,32,256]{3,1,2,0:T(8,128)S(1)} %copy.120, f32[2,32,32,1]{3,1,2,0:T(8,128)S(1)} %copy.112, f32[2,32,32,1]{3,1,2,0:T(8,128)S(1)} %copy-done.2, f32[2,32,1,258]{3,1,2,0:T(8,128)} %collective-permute-done.3, ...), kind=kLoop, calls=%fused_computation.12 | loop fusion | flops 14155776 | bytes 10634240 | tf_op jit(solution)/shard_map/add | solution.py:140
  203.5 28.7 %reduce-scatter.2.cloned.1.call-done = f32[64,384]{1,0:T(8,128)} async-done(((f32[512,384]{1,0:T(8,128)}), f32[64,384]{1,0:T(8,128)}) %reduce-scatter.2.cloned.1.call-update) | async-done | bytes 98320 | tf_op jit(solution)/shard_map/reduce_scatter | solution.py:120
  234.2 1.8 scatter-add.4
  236.0 4.1 %copy.148 = f32[2,32,32,256]{3,2,1,0:T(8,128)} copy(f32[2,32,32,256]{3,1,2,0:T(8,128)} %scatter-add.4) | data formatting | bytes 4194304
  (196 shorter events, 58.2 us)
Async XLA Ops:
  7.2 225.0 %reduce-scatter.2.cloned.1.call-start = ((), (), s32[]{:S(2)}) async-start(), calls=%async_computation.1 | async-start | bytes 884736 | tf_op jit(solution)/shard_map/reduce_scatter | solution.py:120
  9.8 1.5 collective-permute-start.4
  11.3 6.7 %collective-permute-start.5 = (bf16[2,64,512]{2,1,0:T(8,128)(2,1)S(1)}, bf16[2,64,512]{2,1,0:T(8,128)(2,1)S(1)}, u32[]{:S(2)}, u32[]{:S(2)}) collective-permute-start(bf16[2,64,512]{2,1,0:T(8,128)(2,1)S(1)} %pad_maximum_fusion.12), channel_id=1, source_target_pairs={{0,2},{1,3},{2,0},{3,1},{4,6},{5,7},{6,4},{7,5},{8,10},{9,11},{10,... | collective-permute-start | bytes 393224 | tf_op jit(solution)/shard_map/ppermute | solution.py:22
  18.7 13.0 %collective-permute-start.6 = (bf16[4,64,512]{2,1,0:T(8,128)(2,1)S(1)}, bf16[4,64,512]{2,1,0:T(8,128)(2,1)}, u32[]{:S(2)}, u32[]{:S(2)}) collective-permute-start(bf16[4,64,512]{2,1,0:T(8,128)(2,1)S(1)} %pad_maximum_fusion.11), channel_id=1, source_target_pairs={{0,4},{1,5},{2,6},{3,7},{4,0},{5,1},{6,2},{7,3},{8,12},{9,13},{10,... | collective-permute-start | bytes 786440 | tf_op jit(solution)/shard_map/ppermute | solution.py:22
  21.8 17.9 %copy-start.3 = (f32[2,32,32,256]{3,2,1,0:T(8,128)S(1)}, f32[2,32,32,256]{3,2,1,0:T(8,128)}, u32[]{:S(2)}) copy-start(f32[2,32,32,256]{3,2,1,0:T(8,128)} %param.12) | copy-start | bytes 6291460
  24.2 34.8 %collective-permute-start = (f32[2,32,32,1]{2,1,3,0:T(8,128)}, f32[2,32,32,1]{2,1,3,0:T(8,128)}, u32[]{:S(2)}, u32[]{:S(2)}) collective-permute-start(f32[2,32,32,1]{2,1,3,0:T(8,128)} %copy.166), channel_id=1, source_target_pairs={{8,0},{16,8},{24,16},{9,1},{17,9},{25,17},{10,2},{18,10},{26,18},{... | collective-permute-start | bytes 24584 | tf_op jit(solution)/shard_map/ppermute | solution.py:37
  26.6 34.1 %collective-permute-start.1 = (f32[2,32,32,1]{2,1,3,0:T(8,128)}, f32[2,32,32,1]{2,1,3,0:T(8,128)}, u32[]{:S(2)}, u32[]{:S(2)}) collective-permute-start(f32[2,32,32,1]{2,1,3,0:T(8,128)} %copy.167), channel_id=1, source_target_pairs={{0,8},{8,16},{16,24},{1,9},{9,17},{17,25},{2,10},{10,18},{18,26},{... | collective-permute-start | bytes 24584 | tf_op jit(solution)/shard_map/ppermute | solution.py:34
  33.6 12.6 %collective-permute-start.7 = (bf16[8,64,512]{2,1,0:T(8,128)(2,1)}, bf16[8,64,512]{2,1,0:T(8,128)(2,1)}, u32[]{:S(2)}, u32[]{:S(2)}) collective-permute-start(bf16[8,64,512]{2,1,0:T(8,128)(2,1)} %pad_maximum_fusion.10), channel_id=1, source_target_pairs={{0,8},{1,9},{2,10},{3,11},{4,12},{5,13},{6,14},{7,15},{8,0},{9,1},... | collective-permute-start | bytes 1572872 | tf_op jit(solution)/shard_map/ppermute | solution.py:22
  35.4 22.8 %collective-permute-start.9 = (f32[2,1]{1,0:T(2,128)S(1)}, f32[2,1]{1,0:T(2,128)S(1)}, u32[]{:S(2)}, u32[]{:S(2)}) collective-permute-start(f32[2,1]{1,0:T(2,128)S(1)} %get-tuple-element.79), channel_id=1, source_target_pairs={{1,0},{2,1},{3,2},{4,3},{5,4},{6,5},{7,6},{9,8},{10,9},{11,10},{12... | collective-permute-start | bytes 32 | tf_op jit(solution)/shard_map/ppermute | solution.py:37
  36.7 21.5 %collective-permute-start.10 = (f32[2,1]{1,0:T(2,128)S(1)}, f32[2,1]{1,0:T(2,128)S(1)}, u32[]{:S(2)}, u32[]{:S(2)}) collective-permute-start(f32[2,1]{1,0:T(2,128)S(1)} %get-tuple-element.78), channel_id=1, source_target_pairs={{0,1},{1,2},{2,3},{3,4},{4,5},{5,6},{6,7},{8,9},{9,10},{10,11},{11... | collective-permute-start | bytes 32 | tf_op jit(solution)/shard_map/ppermute | solution.py:34
  48.6 46.4 %collective-permute-start.8 = (bf16[16,64,512]{2,1,0:T(8,128)(2,1)}, bf16[16,64,512]{2,1,0:T(8,128)(2,1)}, u32[]{:S(2)}, u32[]{:S(2)}) collective-permute-start(bf16[16,64,512]{2,1,0:T(8,128)(2,1)} %pad_maximum_fusion.9), channel_id=1, source_target_pairs={{0,16},{1,17},{2,18},{3,19},{4,20},{5,21},{6,22},{7,23},{8,24},{9,... | collective-permute-start | bytes 3145736 | tf_op jit(solution)/shard_map/ppermute | solution.py:22
  63.3 31.6 %copy-start.5 = (bf16[8,64,512]{2,1,0:T(8,128)(2,1)S(1)}, bf16[8,64,512]{2,1,0:T(8,128)(2,1)}, u32[]{:S(2)}) copy-start(bf16[8,64,512]{2,1,0:T(8,128)(2,1)} %copy-done.4) | copy-start | bytes 1572868
  63.3 31.6 %copy-start.7 = (bf16[8,64,512]{2,1,0:T(8,128)(2,1)S(1)}, bf16[8,64,512]{2,1,0:T(8,128)(2,1)}, u32[]{:S(2)}) copy-start(bf16[8,64,512]{2,1,0:T(8,128)(2,1)} %copy-done.6) | copy-start | bytes 1572868
  64.9 129.1 %collective-permute-start.2 = (f32[2,32,1,258]{3,1,2,0:T(8,128)}, f32[2,32,1,258]{3,1,2,0:T(8,128)}, u32[]{:S(2)}, u32[]{:S(2)}) collective-permute-start(f32[2,32,1,258]{3,1,2,0:T(8,128)} %get-tuple-element.51), channel_id=1, source_target_pairs={{1,0},{2,1},{3,2},{4,3},{5,4},{6,5},{7,6},{9,8},{10,9},{11,10},{12... | collective-permute-start | bytes 198152 | tf_op jit(solution)/shard_map/ppermute | solution.py:37
  106.9 46.7 %copy-start.28 = (s32[2]{0:T(128)S(1)}, s32[2]{0:T(128)}, u32[]{:S(2)}) copy-start(s32[2]{0:T(128)} %or_bitcast_fusion.1) | copy-start | bytes 28
  107.1 73.1 %copy-start.20 = (s32[3]{0:T(128)S(1)}, s32[3]{0:T(128)}, u32[]{:S(2)}) copy-start(s32[3]{0:T(128)} %or_bitcast_fusion) | copy-start | bytes 40
  107.2 4.3 %collective-permute-start.11 = (f32[2,1]{1,0:T(2,128)S(1)}, f32[2,1]{1,0:T(2,128)S(1)}, u32[]{:S(2)}, u32[]{:S(2)}) collective-permute-start(f32[2,1]{1,0:T(2,128)S(1)} %get-tuple-element.77), channel_id=1, source_target_pairs={{1,0},{2,1},{3,2},{4,3},{5,4},{6,5},{7,6},{9,8},{10,9},{11,10},{12... | collective-permute-start | bytes 32 | tf_op jit(solution)/shard_map/ppermute | solution.py:37
  108.5 3.8 %collective-permute-start.12 = (f32[2,1]{1,0:T(2,128)S(1)}, f32[2,1]{1,0:T(2,128)S(1)}, u32[]{:S(2)}, u32[]{:S(2)}) collective-permute-start(f32[2,1]{1,0:T(2,128)S(1)} %get-tuple-element.76), channel_id=1, source_target_pairs={{0,1},{1,2},{2,3},{3,4},{4,5},{5,6},{6,7},{8,9},{9,10},{10,11},{11... | collective-permute-start | bytes 32 | tf_op jit(solution)/shard_map/ppermute | solution.py:34
  128.6 4.6 %collective-permute-start.13 = (f32[2,1]{1,0:T(2,128)S(1)}, f32[2,1]{1,0:T(2,128)S(1)}, u32[]{:S(2)}, u32[]{:S(2)}) collective-permute-start(f32[2,1]{1,0:T(2,128)S(1)} %get-tuple-element.75), channel_id=1, source_target_pairs={{1,0},{2,1},{3,2},{4,3},{5,4},{6,5},{7,6},{9,8},{10,9},{11,10},{12... | collective-permute-start | bytes 32 | tf_op jit(solution)/shard_map/ppermute | solution.py:37
  129.9 3.8 %collective-permute-start.14 = (f32[2,1]{1,0:T(2,128)S(1)}, f32[2,1]{1,0:T(2,128)S(1)}, u32[]{:S(2)}, u32[]{:S(2)}) collective-permute-start(f32[2,1]{1,0:T(2,128)S(1)} %get-tuple-element.74), channel_id=1, source_target_pairs={{0,1},{1,2},{2,3},{3,4},{4,5},{5,6},{6,7},{8,9},{9,10},{10,11},{11... | collective-permute-start | bytes 32 | tf_op jit(solution)/shard_map/ppermute | solution.py:34
  133.2 29.3 %copy-start.17 = (f32[1,2,4096]{2,0,1:T(1,128)}, f32[1,2,4096]{2,0,1:T(1,128)S(1)}, u32[]{:S(2)}) copy-start(f32[1,2,4096]{2,0,1:T(1,128)S(1)} %copy.130) | copy-start | bytes 98308
  135.5 58.5 %collective-permute-start.3 = (f32[2,32,1,258]{3,1,2,0:T(8,128)}, f32[2,32,1,258]{3,1,2,0:T(8,128)}, u32[]{:S(2)}, u32[]{:S(2)}) collective-permute-start(f32[2,32,1,258]{3,1,2,0:T(8,128)} %get-tuple-element.50), channel_id=1, source_target_pairs={{0,1},{1,2},{2,3},{3,4},{4,5},{5,6},{6,7},{8,9},{9,10},{10,11},{11... | collective-permute-start | bytes 198152 | tf_op jit(solution)/shard_map/ppermute | solution.py:34
  157.2 4.3 %collective-permute-start.15 = (f32[2,1]{1,0:T(2,128)S(1)}, f32[2,1]{1,0:T(2,128)S(1)}, u32[]{:S(2)}, u32[]{:S(2)}) collective-permute-start(f32[2,1]{1,0:T(2,128)S(1)} %get-tuple-element.73), channel_id=1, source_target_pairs={{1,0},{2,1},{3,2},{4,3},{5,4},{6,5},{7,6},{9,8},{10,9},{11,10},{12... | collective-permute-start | bytes 32 | tf_op jit(solution)/shard_map/ppermute | solution.py:37
  158.5 3.8 %collective-permute-start.16 = (f32[2,1]{1,0:T(2,128)S(1)}, f32[2,1]{1,0:T(2,128)S(1)}, u32[]{:S(2)}, u32[]{:S(2)}) collective-permute-start(f32[2,1]{1,0:T(2,128)S(1)} %get-tuple-element.72), channel_id=1, source_target_pairs={{0,1},{1,2},{2,3},{3,4},{4,5},{5,6},{6,7},{8,9},{9,10},{10,11},{11... | collective-permute-start | bytes 32 | tf_op jit(solution)/shard_map/ppermute | solution.py:34
  (24 other events, 138.9 us)
Sparse Core Ops, SparseCore 0:
  194.2 37.9 reduce-scatter.1
